TPU v7x, 32 devices: a whole 2x2x4 slice. The times are simulated.
32 devices in a mesh: row: 4 (over z), col: 8 (over y, x, core).
Axes of the slice: x: 2, y: 2, z: 4, core: 2. Of those that a mesh axis runs over, the one named last changes fastest.
Arguments:
- a_matrix: bfloat16 [8192, 8192], P('row', 'col'), may hold values from -6 to 6
- a_flags: int32 [64, 64], P('row', 'col'), may hold values from 0 to 1, as said below
- b_matrix: bfloat16 [8192, 16384], P('row', 'col'), may hold values from -0.1875 to 0.1875
- b_flags: int32 [64, 128], P('row', 'col'), may hold values from 0 to 1, as said below
- sections: int32 [2], replicated, may hold values from 0 to 7
Outputs:
- packed: bfloat16 [8192, 16384], P('row', 'col')
- tile_place: int32 [64, 128], P('row', 'col')
Inputs may be any that keep to these rules, and one draw needn't show every extreme that they name: `a_flags`: 0 or 1; the 16 x 8 tiles of one device hold at most 64 ones, and some device holds exactly 64. `b_flags`: 0 or 1; each aligned block of 8 x 16 tiles holds at most 64 ones, and some block exactly 64.
All inputs are finite; a program needn't handle non-finite values.
Results may differ from a plain program's by a relative error of at most 0.001.
Values may be sent and summed in bfloat16 or wider, within the bound.
No kernel may reach another device: no remote copies, remote signals or barrier semaphores. Data moves between devices by JAX's collectives and lax.ppermute only.
A program may use at most 128 MiB of HBM per device.

v0:
```python
import jax
import jax.numpy as jnp
from jax import lax
from jax.sharding import PartitionSpec as P

TILE = 128
SECTIONS = 2
MOST = 64


def spread(value, axis, source):
    kept = jnp.where(lax.axis_index(axis) == source, value, 0).astype(value.dtype)
    return lax.psum(kept, axis)


def prefix(value, axis, combine, identity):
    length, position = (lax.axis_size(axis), lax.axis_index(axis))
    everything = lax.all_gather(value, axis)
    start = jnp.broadcast_to(jnp.asarray(identity, value.dtype), value.shape)

    def lap(k, before):
        reached = k < position
        new = combine(before, everything[k])
        return jnp.where(reached, new, before)

    return lax.fori_loop(0, length, lap, start)


def to_tiles(matrix, tile_rows, tile_cols):
    return (
        matrix.reshape(tile_rows, TILE, tile_cols, TILE)
        .transpose(0, 2, 1, 3)
        .reshape(tile_rows * tile_cols, TILE, TILE)
    )


def from_tiles(tiles, tile_rows, tile_cols):
    return (
        tiles.reshape(tile_rows, tile_cols, TILE, TILE)
        .transpose(0, 2, 1, 3)
        .reshape(tile_rows * TILE, tile_cols * TILE)
    )


def mask_tiles(matrix, flags, tile_rows, tile_cols):
    shaped = matrix.reshape(tile_rows, TILE, tile_cols, TILE)
    shaped = shaped * flags[:, None, :, None]
    return shaped.reshape(tile_rows * TILE, tile_cols * TILE)


def compact(tiles, flags_flat, capacity):
    rank_of = jnp.cumsum(flags_flat) - 1
    slot_ids = jnp.arange(capacity, dtype=jnp.int32)
    matched = (flags_flat[None, :] == 1) & (rank_of[None, :] == slot_ids[:, None])
    source = jnp.sum(
        jnp.where(matched, jnp.arange(flags_flat.shape[0], dtype=jnp.int32)[None, :], 0), axis=1
    )
    is_valid = jnp.any(matched, axis=1)
    return jnp.take(tiles, source, axis=0) * is_valid.astype(tiles.dtype)[:, None, None]


def expand(packed_tiles, flags_flat, capacity):
    rank_of = jnp.cumsum(flags_flat) - 1
    position = jnp.where(flags_flat == 1, rank_of, capacity)
    extended = jnp.concatenate(
        [packed_tiles, jnp.zeros((1, TILE, TILE), packed_tiles.dtype)], axis=0
    )
    return jnp.take(extended, position, axis=0)


def add_up(earlier, later):
    return earlier + later


def shards(a_matrix, a_flags, b_matrix, b_flags, sections):
    tile_rows, panel_cols = a_flags.shape
    tile_cols = b_flags.shape[1]
    row_ratio = lax.axis_size("col") // lax.axis_size("row")
    panel_width = panel_cols * TILE
    a_send_flags = a_flags.astype(jnp.bfloat16)
    product = jnp.zeros((tile_rows * TILE, tile_cols * TILE), jnp.float32)
    intersection = jnp.zeros((tile_rows, tile_cols), jnp.float32)
    for step_index in range(SECTIONS):
        section = sections[step_index]
        owner_row = section // row_ratio
        start_tile = section % row_ratio * panel_cols
        b_panel = lax.dynamic_slice_in_dim(b_matrix, start_tile * TILE, panel_width, 0)
        b_panel_flags = lax.dynamic_slice_in_dim(b_flags, start_tile, panel_cols, 0)
        b_send_flags = b_panel_flags.astype(jnp.bfloat16)
        a_packed = compact(to_tiles(a_matrix, tile_rows, panel_cols), a_flags.reshape(-1), MOST)
        b_packed = compact(
            to_tiles(b_panel, panel_cols, tile_cols), b_panel_flags.reshape(-1), MOST
        )
        a_recv, a_got_flags = (
            spread(a_packed, "col", section),
            spread(a_send_flags, "col", section),
        )
        b_recv, b_got_flags = (
            spread(b_packed, "row", owner_row),
            spread(b_send_flags, "row", owner_row),
        )
        a_got = from_tiles(
            expand(a_recv, a_got_flags.astype(jnp.int32).reshape(-1), MOST), tile_rows, panel_cols
        )
        b_got = from_tiles(
            expand(b_recv, b_got_flags.astype(jnp.int32).reshape(-1), MOST), panel_cols, tile_cols
        )
        a_masked = mask_tiles(a_got, a_got_flags, tile_rows, panel_cols)
        b_masked = mask_tiles(b_got, b_got_flags, panel_cols, tile_cols)
        product = product + jnp.dot(a_masked, b_masked, preferred_element_type=jnp.float32)
        intersection = intersection + jnp.dot(
            a_got_flags.astype(jnp.float32),
            b_got_flags.astype(jnp.float32),
            precision=lax.Precision.HIGHEST,
        )
    occupied = (intersection > 0.5).astype(jnp.int32).reshape(-1)
    filled = jnp.sum(occupied).reshape(1)
    zero_count = jnp.zeros((1,), jnp.int32)
    offset = prefix(filled, ("row", "col"), add_up, zero_count)
    tiles = to_tiles(product.astype(jnp.bfloat16), tile_rows, tile_cols)
    packed = from_tiles(compact(tiles, occupied, tile_rows * tile_cols), tile_rows, tile_cols)
    slot_ids = jnp.arange(tile_rows * tile_cols, dtype=jnp.int32)
    places = jnp.where(slot_ids < filled[0], offset[0] + slot_ids, -1).astype(jnp.int32)
    return (packed, places.reshape(tile_rows, tile_cols))


def solution(mesh):
    return jax.shard_map(
        shards,
        mesh=mesh,
        in_specs=(P("row", "col"), P("row", "col"), P("row", "col"), P("row", "col"), P()),
        out_specs=(P("row", "col"), P("row", "col")),
        check_vma=False,
    )
```

profile of v0, /device:TPU:0, one launch (start us, length us, event | category | flops | bytes accessed | tf_op | source)
XLA Modules:
  0.0 386.5 jit_solution(5069654762923967390)
XLA Ops:
  7.2 0.8 copy.70
  8.0 0.7 broadcast_compare_fusion.7
  9.5 1.3 fusion.23
  12.2 3.3 copy.90
  15.8 3.3 copy.72
  19.1 3.1 gather_fusion.1
  22.3 2.4 broadcast_select_fusion.4
  30.5 9.1 %dynamic-slice_bitcast_fusion = (bf16[128,8,16,128]{3,1,2,0:T(8,128)(2,1)S(1)}, bf16[128,8,16,128]{3,1,2,0:T(8,128)(2,1)}) fusion(bf16[2048,2048]{1,0:T(8,128)(2,1)} %param.13, s32[]{:T(128)S(6)} %select_n.201, s32[]{:T(128)S(6)} %select_n.193), kind=kLoop, calls=%fused_computation.29 | loop fusion | bytes 16777224
  39.6 1.4 copy.95
  41.0 0.7 bitcast_bitcast_fusion
  41.8 3.1 copy.86
  45.6 3.7 copy.92
  49.3 0.7 bitcast_bitcast_fusion.1
  50.0 3.2 copy.77
  53.7 3.1 gather_fusion.6
  56.9 4.7 %gather_fusion.3 = bf16[64,128,128]{2,1,0:T(8,128)(2,1)} fusion(bf16[128,128,128]{2,1,0:T(8,128)(2,1)} %bitcast.100, s32[1024]{0:T(1024)S(1)} %pad_clamp_fusion.5), kind=kCustom, calls=%fused_computation.2.clone | custom fusion | bytes 4194560 | tf_op jit(solution)/shard_map/jit(_take)/gather | solution.py:59
  61.6 1.7 fusion.10
  63.9 1.7 fusion.11
  65.6 13.2 %all-reduce.7 = (bf16[8,16]{1,0:T(8,128)(2,1)S(1)}, bf16[8,16]{1,0:T(8,128)(2,1)S(1)}) all-reduce(bf16[8,16]{1,0:T(8,128)(2,1)S(1)} %get-tuple-element.116, bf16[8,16]{1,0:T(8,128)(2,1)S(1)} %get-tuple-element.108), channel_id=1, replica_groups=mesh['row'=4,'col'=8] {'row'}, use_global_device_ids=true, to_apply=%region_1.2 | all-reduce | flops 256 | bytes 1024 | tf_op jit(solution)/shard_map/psum | solution.py:13
  78.8 11.8 %all-reduce.5 = (bf16[16,8]{0,1:T(8,128)(2,1)S(1)}, bf16[16,8]{0,1:T(8,128)(2,1)S(1)}) all-reduce(bf16[16,8]{0,1:T(8,128)(2,1)S(1)} %get-tuple-element.119, bf16[16,8]{0,1:T(8,128)(2,1)S(1)} %get-tuple-element.118), channel_id=1, replica_groups=mesh['row'=4,'col'=8] {'col'}, use_global_device_ids=true, to_apply=%region_0.1 | all-reduce | flops 256 | bytes 1024 | tf_op jit(solution)/shard_map/psum | solution.py:13
  91.3 0.7 reduce_sum.59
  94.3 0.7 dynamic-update-slice
  95.1 40.6 %all-reduce.4 = s32[32]{0:T(128)S(1)} all-reduce(s32[32]{0:T(128)S(1)} %dynamic-update-slice), channel_id=1, replica_groups=mesh['row'=4,'col'=8] {'row','col'}, use_global_device_ids=true, to_apply=%add.4 | all-reduce | flops 32 | bytes 256
  136.2 44.6 %while.13 = (s32[]{:T(128)}, s32[1]{0:T(128)}, s32[]{:T(128)}, s32[32,1]{0,1:T(1,128)S(1)}, s32[]{:T(128)}) while((s32[]{:T(128)}, s32[1]{0:T(128)}, s32[]{:T(128)}, s32[32,1]{0,1:T(1,128)S(1)}, s32[]{:T(128)}) %tuple.62), condition=%wide.region_27.30_spmd, body=%wide.region_26.29_spmd.sunk | while | flops 5 | bytes 107 | solution.py:26
  136.2 0.7 constant_dynamic-slice_fusion.6
  137.6 0.7 constant_dynamic-slice_fusion.6
  139.0 0.7 constant_dynamic-slice_fusion.6
  140.4 0.7 constant_dynamic-slice_fusion.6
  141.8 0.7 constant_dynamic-slice_fusion.6
  143.1 0.7 constant_dynamic-slice_fusion.6
  144.5 0.7 constant_dynamic-slice_fusion.6
  145.9 0.7 constant_dynamic-slice_fusion.6
  147.3 0.7 constant_dynamic-slice_fusion.6
  148.7 0.7 constant_dynamic-slice_fusion.6
  150.0 0.7 constant_dynamic-slice_fusion.6
  151.4 0.7 constant_dynamic-slice_fusion.6
  152.8 0.7 constant_dynamic-slice_fusion.6
  154.2 0.7 constant_dynamic-slice_fusion.6
  181.4 1.2 add_select_fusion
  182.6 1.9 concatenate.12
  184.9 1.5 concatenate.14
  186.4 3.1 gather_fusion.2
  189.5 4.6 %gather_fusion.5 = bf16[128,128,128]{2,1,0:T(8,128)(2,1)} fusion(bf16[65,128,128]{2,1,0:T(8,128)(2,1)} %concatenate.14, s32[1024]{0:T(1024)S(1)} %pad_clamp_fusion.3), kind=kCustom, calls=%fused_computation.5.clone | custom fusion | bytes 8389120 | tf_op jit(solution)/shard_map/jit(_take)/gather | solution.py:68
  194.1 3.2 broadcast_select_fusion.3
  197.3 1.0 copy-done
  198.8 4.4 %copy_multiply_fusion.3 = bf16[16,8,128,128]{3,1,2,0:T(8,128)(2,1)} fusion(bf16[16,8,128,128]{3,2,1,0:T(8,128)(2,1)S(1)} %bitcast.97, bf16[16,8]{1,0:T(8,128)(2,1)S(1)} %copy.73), kind=kLoop, calls=%fused_computation.28 | loop fusion | flops 2097152 | bytes 8388864 | tf_op jit(solution)/shard_map/mul | solution.py:47
  203.2 4.4 %copy_multiply_fusion.1 = bf16[16,8,128,128]{3,1,2,0:T(8,128)(2,1)} fusion(bf16[16,8,128,128]{3,2,1,0:T(8,128)(2,1)S(1)} %bitcast.98, bf16[16,8]{1,0:T(8,128)(2,1)S(1)} %copy.82), kind=kLoop, calls=%fused_computation.26 | loop fusion | flops 2097152 | bytes 8388864 | tf_op jit(solution)/shard_map/mul | solution.py:47
  207.5 59.3 %all-reduce.14.cloned.1.call-done = (bf16[64,128,128]{2,1,0:T(8,128)(2,1)}, bf16[64,128,128]{2,1,0:T(8,128)(2,1)}) async-done(((bf16[64,128,128]{2,1,0:T(8,128)(2,1)}, bf16[64,128,128]{2,1,0:T(8,128)(2,1)}), (bf16[64,128,128]{2,1,0:T(8,128)(2,1)}, bf16[64,128,128]{2,1,0:T(8,128)(2,1)})) %all-reduce.14.cloned.1.call-update) | async-done | bytes 4194320 | tf_op jit(solution)/shard_map/psum | solution.py:13
  266.9 1.8 concatenate.13
  268.6 3.1 gather_fusion.4
  271.7 2.6 broadcast_select_fusion.2
  274.4 4.3 %copy_multiply_fusion.2 = bf16[8,16,128,128]{3,1,2,0:T(8,128)(2,1)} fusion(bf16[8,16,128,128]{3,2,1,0:T(8,128)(2,1)S(1)} %bitcast.92, bf16[8,16]{1,0:T(8,128)(2,1)S(1)} %get-tuple-element.96), kind=kLoop, calls=%fused_computation.27 | loop fusion | flops 2097152 | bytes 8388864 | tf_op jit(solution)/shard_map/mul | solution.py:47
  278.9 3.2 gather_fusion.7
  282.1 2.6 broadcast_select_fusion
  284.8 2.3 copy_multiply_fusion
  287.1 1.1 copy-done.3
  288.2 11.7 %fusion.5 = f32[2048,2048]{1,0:T(8,128)} fusion(bf16[128,8,16,128]{3,2,1,0:T(8,128)(2,1)S(1)} %bitcast.103, bf16[256,8,8,128]{3,2,1,0:T(8,128)(2,1)S(1)} %bitcast.106), kind=kOutput, calls=%fused_computation.18 | convolution fusion | flops 8589934592 | bytes 25165824 | tf_op jit(solution)/shard_map/dot_general | solution.py:110
  299.9 16.3 %fusion = bf16[256,8,16,128]{3,1,2,0:T(8,128)(2,1)} fusion(f32[2048,2048]{1,0:T(8,128)} %fusion.5, bf16[128,8,16,128]{3,2,1,0:T(8,128)(2,1)S(1)} %bitcast.104, bf16[256,8,8,128]{3,2,1,0:T(8,128)(2,1)} %bitcast.107), kind=kOutput, calls=%fused_computation.10 | convolution fusion | flops 8598323200 | bytes 33554432 | tf_op jit(solution)/shard_map/dot_general | solution.py:110
  316.1 9.8 %copy.97 = bf16[256,8,16,128]{3,2,1,0:T(8,128)(2,1)} copy(bf16[256,8,16,128]{3,1,2,0:T(8,128)(2,1)} %fusion) | data formatting | bytes 16777216
  325.9 9.3 %copy.88 = bf16[16,128,16,128]{3,1,2,0:T(8,128)(2,1)} copy(bf16[16,128,16,128]{3,2,1,0:T(8,128)(2,1)} %bitcast.90) | data formatting | bytes 16777216 | tf_op jit(solution)/shard_map/reshape | solution.py:31
  335.2 12.0 %gather_fusion = bf16[256,128,128]{2,1,0:T(8,128)(2,1)} fusion(bf16[256,128,128]{2,1,0:T(8,128)(2,1)} %bitcast.89, s32[1024]{0:T(1024)S(1)} %pad_clamp_fusion), kind=kCustom, calls=%fused_computation.7 | custom fusion | bytes 16778240 | tf_op jit(solution)/shard_map/jit(_take)/gather | solution.py:59
  347.2 7.5 %multiply_bitcast_fusion = bf16[16,128,16,128]{3,1,2,0:T(8,128)(2,1)} fusion(bf16[16,16,128,128]{3,2,1,0:T(8,128)(2,1)} %bitcast.88, pred[16,16]{1,0:T(8,128)(4,1)S(1)} %compare_and_fusion, bf16[16,16]{1,0:T(8,128)(2,1)S(1)} %reshape.414), kind=kLoop, calls=%fused_computation.12 | loop fusion | flops 8388608 | bytes 16777984 | tf_op jit(solution)/shard_map/transpose | solution.py:40
  354.7 13.7 %copy.89 = bf16[16,128,16,128]{3,2,1,0:T(8,128)(2,1)} copy(bf16[16,128,16,128]{3,1,2,0:T(8,128)(2,1)} %multiply_bitcast_fusion) | data formatting | bytes 16777216 | tf_op jit(solution)/shard_map/transpose | solution.py:40
  368.4 11.1 %copy.120 = bf16[256,8,16,128]{3,1,2,0:T(8,128)(2,1)} copy(bf16[256,8,16,128]{3,2,1,0:T(8,128)(2,1)} %bitcast.91) | data formatting | bytes 16777216
  (127 shorter events, 20.5 us)
Async XLA Ops:
  7.2 175.5 %all-reduce.12.cloned.1.call-start = ((), (), s32[]{:S(2)}) async-start(), calls=%async_computation | async-start | bytes 8388608 | tf_op jit(solution)/shard_map/psum | solution.py:13
  22.3 8.0 %copy-start.7 = (s32[16,16]{1,0:T(8,128)S(1)}, s32[16,16]{1,0:T(8,128)}, u32[]{:S(2)}) copy-start(s32[16,16]{1,0:T(8,128)} %param.14) | copy-start | bytes 3076
  24.7 242.2 %all-reduce.14.cloned.1.call-start = ((), (), s32[]{:S(2)}) async-start(), calls=%async_computation.1 | async-start | bytes 8388608 | tf_op jit(solution)/shard_map/psum | solution.py:13
  61.6 2.3 copy-start.1
  63.9 14.9 %copy-start.6 = (s32[16,8]{0,1:T(8,128)S(1)}, s32[16,8]{0,1:T(8,128)}, u32[]{:S(2)}) copy-start(s32[16,8]{0,1:T(8,128)} %param.12) | copy-start | bytes 1540
  182.6 2.3 copy-start.4
  194.1 4.2 %copy-start = (bf16[128,128,128]{2,1,0:T(8,128)(2,1)S(1)}, bf16[128,128,128]{2,1,0:T(8,128)(2,1)}, u32[]{:S(2)}) copy-start(bf16[128,128,128]{2,1,0:T(8,128)(2,1)} %gather_fusion.5) | copy-start | bytes 12582916
  274.4 4.3 %copy-start.5 = (bf16[64,128,128]{2,1,0:T(8,128)(2,1)S(1)}, bf16[64,128,128]{2,1,0:T(8,128)(2,1)}, u32[]{:S(2)}) copy-start(bf16[64,128,128]{2,1,0:T(8,128)(2,1)} %get-tuple-element.99) | copy-start | bytes 6291460
  284.7 2.3 copy-start.2
  284.8 3.5 copy-start.3
Sparse Core Ops, SparseCore 0:
  24.8 84.2 all-reduce.11
  111.5 155.3 all-reduce.13
where the time goes:
time: 391 us; the launch traced here: 387 us
  local copies, waits for them, and re-layouts  145 us (37%)
  blocking collectives  65.6 us (17%)
  waiting for transfers between devices  59.4 us (15%)
  other arithmetic  43.6 us (11%)
  matrix products  28.3 us (7%)
  loops' own time  23.3 us (6%)
  between operations  21.6 us (6%)
    psum x2, waiting for transfers between devices, spread(): return lax.psum(kept, axis)  59.3 us
    unnamed x25, local copies, waits for them, and re-layouts  42.9 us
    unnamed x1, blocking collectives  40.6 us
    dot_general x2, matrix products, shards(): jnp.dot(a_masked, b_masked, preferred_element_type=jnp.float32)  27.9 us
    psum x2, blocking collectives, spread(): return lax.psum(kept, axis)  25 us
    another operation x1, loops' own time, prefix(): return lax.fori_loop(0, length, lap, start)  23.3 us
    gather x4, local copies, waits for them, and re-layouts, compact(): jnp.take(tiles, source, axis=0)  23 us
    dynamic_slice x32, local copies, waits for them, and re-layouts, lap(): new = combine(before, everything[k])  21.3 us
  transfers between devices with their start and end apart: 2, of which 1 were waited for; matrix products, arithmetic and copies ran while one was open for 22% of the time, Pallas kernels for 0%

commit v1 on v0

--- a/solution.py
+++ b/solution.py
@@ -10,7 +10,7 @@
 
 def spread(value, axis, source):
     kept = jnp.where(lax.axis_index(axis) == source, value, 0).astype(value.dtype)
-    return lax.psum(kept, axis)
+    return jnp.sum(lax.all_gather(kept, axis), axis=0)
 
 
 def prefix(value, axis, combine, identity):

time: 391 us -> 663 us (1.70)
  waiting for transfers between devices: 59.4 us -> 258 us
  blocking collectives: 65.6 us -> 97.7 us
  other arithmetic: 43.6 us -> 67.7 us
  local copies, waits for them, and re-layouts: 145 us -> 159 us
    all_gather x0 -> x4, waiting for transfers between devices: none -> 258 us  [spread(): return jnp.sum(lax.all_gather(kept, axis), axis=0)]
    psum x2 -> x0, waiting for transfers between devices: 59.3 us -> none  [spread(): return lax.psum(kept, axis)]
    all_gather x0 -> x4, blocking collectives: none -> 49.6 us  [spread(): return jnp.sum(lax.all_gather(kept, axis), axis=0)]
    reduce_sum x0 -> x8, other arithmetic: none -> 36.4 us  [spread(): return jnp.sum(lax.all_gather(kept, axis), axis=0)]
    psum x2 -> x0, blocking collectives: 25 us -> none  [spread(): return lax.psum(kept, axis)]
    mul x0 -> x4, local copies, waits for them, and re-layouts: none -> 19.1 us  [mask_tiles(): shaped = shaped * flags[:, None, :, None]]
    mul x4, other arithmetic: 15.3 us -> 1.36 us  [mask_tiles(): shaped = shaped * flags[:, None, :, None]]
    unnamed x1, blocking collectives: 40.6 us -> 48.1 us
  transfers between devices with their start and end apart: 2 -> 4, of which waited for: 1 -> 3; matrix products, arithmetic and copies ran while one was open for 22% -> 16% of each run, Pallas kernels for 0% -> 0%
where the time goes in v1:
time: 663 us; the launch traced here: 654 us
  waiting for transfers between devices  258 us (39%)
  local copies, waits for them, and re-layouts  159 us (24%)
  blocking collectives  97.7 us (15%)
  other arithmetic  67.7 us (10%)
  matrix products  28.5 us (4%)
  between operations  21.4 us (3%)
  loops' own time  21.3 us (3%)
    all_gather x4, waiting for transfers between devices, spread(): return jnp.sum(lax.all_gather(kept, axis), axis=0)  258 us
    all_gather x4, blocking collectives, spread(): return jnp.sum(lax.all_gather(kept, axis), axis=0)  49.6 us
    unnamed x1, blocking collectives  48.1 us
    unnamed x17, local copies, waits for them, and re-layouts  38.7 us
    reduce_sum x8, other arithmetic, spread(): return jnp.sum(lax.all_gather(kept, axis), axis=0)  36.4 us
    dot_general x2, matrix products, shards(): jnp.dot(a_masked, b_masked, preferred_element_type=jnp.float32)  28.1 us
    gather x4, local copies, waits for them, and re-layouts, compact(): jnp.take(tiles, source, axis=0)  21.8 us
    another operation x1, loops' own time, prefix(): return lax.fori_loop(0, length, lap, start)  21.3 us
  transfers between devices with their start and end apart: 4, of which 3 were waited for; matrix products, arithmetic and copies ran while one was open for 16% of the time, Pallas kernels for 0%

profile of v1, /device:TPU:0, one launch (start us, length us, event | category | flops | bytes accessed | tf_op | source)
XLA Modules:
  0.0 654.4 jit_solution(12607417675712547584)
XLA Ops:
  7.2 1.3 fusion.23
  13.9 0.7 convert_select_fusion
  16.0 8.3 %dynamic-slice_bitcast_fusion = (bf16[128,8,16,128]{3,1,2,0:T(8,128)(2,1)S(1)}, bf16[128,8,16,128]{3,1,2,0:T(8,128)(2,1)}) fusion(bf16[2048,2048]{1,0:T(8,128)(2,1)} %param.13, s32[]{:T(128)S(6)} %select_n.201, s32[]{:T(128)S(6)} %select_n.193), kind=kLoop, calls=%fused_computation.26 | loop fusion | bytes 16777224
  24.3 1.4 copy.115
  25.7 0.7 bitcast_bitcast_fusion
  26.4 3.1 copy.106
  29.5 3.1 gather_fusion.6
  32.6 1.6 fusion.10
  34.5 3.6 copy.112
  38.1 0.7 bitcast_bitcast_fusion.1
  38.8 3.2 copy.97
  42.0 3.4 gather_fusion.3
  45.4 1.7 fusion.11
  49.8 3.4 copy.110
  53.6 3.3 copy.92
  57.0 3.2 gather_fusion.1
  60.2 2.4 broadcast_select_fusion.4
  63.2 10.5 %all-gather.9 = bf16[8,16,8]{1,2,0:T(8,128)(2,1)S(1)} all-gather(bf16[1,16,8]{1,2,0:T(8,128)(2,1)S(1)} %get-tuple-element.110), channel_id=4, replica_groups=mesh['row'=4,'col'=8] {'col'}, dimensions={0}, use_global_device_ids=true | all-gather | bytes 2304 | tf_op jit(solution)/shard_map/all_gather | solution.py:13
  73.7 8.9 %all-gather.8 = bf16[8,16,8]{1,2,0:T(8,128)(2,1)S(1)} all-gather(bf16[1,16,8]{1,2,0:T(8,128)(2,1)S(1)} %get-tuple-element.111), channel_id=2, replica_groups=mesh['row'=4,'col'=8] {'col'}, dimensions={0}, use_global_device_ids=true | all-gather | bytes 2304 | tf_op jit(solution)/shard_map/all_gather | solution.py:13
  82.6 16.0 %all-gather.3 = bf16[32,16]{1,0:T(8,128)(2,1)S(1)} all-gather(bf16[8,16]{1,0:T(8,128)(2,1)S(1)} %get-tuple-element.96), channel_id=5, replica_groups=mesh['row'=4,'col'=8] {'row'}, dimensions={0}, use_global_device_ids=true | all-gather | bytes 1280 | tf_op jit(solution)/shard_map/all_gather | solution.py:13
  98.6 14.2 %all-gather.1 = bf16[32,16]{1,0:T(8,128)(2,1)S(1)} all-gather(bf16[8,16]{1,0:T(8,128)(2,1)S(1)} %get-tuple-element.108), channel_id=3, replica_groups=mesh['row'=4,'col'=8] {'row'}, dimensions={0}, use_global_device_ids=true | all-gather | bytes 1280 | tf_op jit(solution)/shard_map/all_gather | solution.py:13
  113.2 0.7 reduce_sum.163
  113.9 0.8 dynamic-update-slice
  114.7 48.1 %all-reduce.4 = s32[32]{0:T(128)S(1)} all-reduce(s32[32]{0:T(128)S(1)} %dynamic-update-slice), channel_id=1, replica_groups=mesh['row'=4,'col'=8] {'row','col'}, use_global_device_ids=true, to_apply=%add.4 | all-reduce | flops 32 | bytes 256
  166.0 41.7 %while.13 = (s32[]{:T(128)}, s32[1]{0:T(128)}, s32[]{:T(128)}, s32[32,1]{0,1:T(1,128)S(1)}, s32[]{:T(128)}) while((s32[]{:T(128)}, s32[1]{0:T(128)}, s32[]{:T(128)}, s32[32,1]{0,1:T(1,128)S(1)}, s32[]{:T(128)}) %tuple.64), condition=%wide.region_27.30_spmd, body=%wide.region_26.29_spmd.sunk | while | flops 5 | bytes 115 | solution.py:26
  167.4 0.6 constant_dynamic-slice_fusion.6
  169.9 0.6 constant_dynamic-slice_fusion.6
  173.8 0.6 constant_dynamic-slice_fusion.6
  176.4 0.6 constant_dynamic-slice_fusion.6
  179.0 0.6 constant_dynamic-slice_fusion.6
  182.9 0.6 constant_dynamic-slice_fusion.6
  185.5 0.6 constant_dynamic-slice_fusion.6
  208.3 1.3 add_select_fusion
  209.6 7.2 %reduce_sum.161 = bf16[64,128,128]{2,1,0:T(8,128)(2,1)} reduce(bf16[4,64,128,128]{3,2,1,0:T(8,128)(2,1)} %bitcast.120, bf16[]{:T(256)} %constant.142.clone.1), dimensions={0}, to_apply=%region_22.25 | reduce | flops 3145728 | bytes 10485762 | tf_op jit(solution)/shard_map/reduce_sum | solution.py:13
  216.8 1.8 concatenate.15
  218.6 3.1 gather_fusion.7
  221.7 2.6 broadcast_select_fusion
  224.6 4.8 copy.107
  229.4 108.0 %all-gather.17.cloned.1.call-done = bf16[256,128,128]{2,1,0:T(8,128)(2,1)} async-done(((bf16[64,128,128]{2,1,0:T(8,128)(2,1)}), bf16[256,128,128]{2,1,0:T(8,128)(2,1)}) %all-gather.17.cloned.1.call-update) | async-done | bytes 8388624 | tf_op jit(solution)/shard_map/all_gather | solution.py:13
  337.4 7.2 %reduce_sum.158 = bf16[64,128,128]{2,1,0:T(8,128)(2,1)} reduce(bf16[4,64,128,128]{3,2,1,0:T(8,128)(2,1)} %bitcast.121, bf16[]{:T(256)} %constant.142.clone.1), dimensions={0}, to_apply=%region_15.18 | reduce | flops 3145728 | bytes 10485762 | tf_op jit(solution)/shard_map/reduce_sum | solution.py:13
  344.6 2.2 concatenate.13
  346.8 3.1 gather_fusion.4
  349.9 2.6 broadcast_select_fusion.2
  352.9 5.3 copy.98
  358.1 69.1 %all-gather.19.cloned.1.call-done = bf16[512,128,128]{2,1,0:T(8,128)(2,1)} async-done(((bf16[64,128,128]{2,1,0:T(8,128)(2,1)}), bf16[512,128,128]{2,1,0:T(8,128)(2,1)}) %all-gather.19.cloned.1.call-update) | async-done | bytes 16777232 | tf_op jit(solution)/shard_map/all_gather | solution.py:13
  427.3 11.1 %reduce_sum.159 = bf16[64,128,128]{2,1,0:T(8,128)(2,1)} reduce(bf16[8,64,128,128]{3,2,1,0:T(8,128)(2,1)} %bitcast.110, bf16[]{:T(256)} %constant.142.clone.1), dimensions={0}, to_apply=%region_17.20 | reduce | flops 7340032 | bytes 18874370 | tf_op jit(solution)/shard_map/reduce_sum | solution.py:13
  438.4 80.4 %all-gather.15.cloned.1.call-done = bf16[512,128,128]{2,1,0:T(8,128)(2,1)} async-done(((bf16[64,128,128]{2,1,0:T(8,128)(2,1)}), bf16[512,128,128]{2,1,0:T(8,128)(2,1)}) %all-gather.15.cloned.1.call-update) | async-done | bytes 16777232 | tf_op jit(solution)/shard_map/all_gather | solution.py:13
  518.8 10.8 %reduce_sum.156 = bf16[64,128,128]{2,1,0:T(8,128)(2,1)} reduce(bf16[8,64,128,128]{3,2,1,0:T(8,128)(2,1)} %bitcast.111, bf16[]{:T(256)} %constant.142.clone.1), dimensions={0}, to_apply=%region_10.12 | reduce | flops 7340032 | bytes 18874370 | tf_op jit(solution)/shard_map/reduce_sum | solution.py:13
  529.6 1.9 concatenate.12
  531.8 1.5 concatenate.14
  533.3 4.6 gather_fusion.5
  537.9 2.6 broadcast_select_fusion.1
  540.9 5.5 copy.103
  546.4 3.0 gather_fusion.2
  549.4 2.6 broadcast_select_fusion.3
  552.4 3.6 copy.94
  556.0 11.9 %fusion.5 = f32[2048,2048]{1,0:T(8,128)} fusion(bf16[128,8,16,128]{3,2,1,0:T(8,128)(2,1)S(1)} %bitcast.125, bf16[256,8,8,128]{3,2,1,0:T(8,128)(2,1)S(1)} %bitcast.127), kind=kOutput, calls=%fused_computation.18 | convolution fusion | flops 8589934592 | bytes 25165824 | tf_op jit(solution)/shard_map/dot_general | solution.py:110
  567.9 16.3 %fusion = bf16[256,8,16,128]{3,1,2,0:T(8,128)(2,1)} fusion(f32[2048,2048]{1,0:T(8,128)} %fusion.5, bf16[128,8,16,128]{3,2,1,0:T(8,128)(2,1)S(1)} %bitcast.124, bf16[256,8,8,128]{3,2,1,0:T(8,128)(2,1)} %bitcast.126), kind=kOutput, calls=%fused_computation.10 | convolution fusion | flops 8598323200 | bytes 33554432 | tf_op jit(solution)/shard_map/dot_general | solution.py:110
  584.2 9.8 %copy.117 = bf16[256,8,16,128]{3,2,1,0:T(8,128)(2,1)} copy(bf16[256,8,16,128]{3,1,2,0:T(8,128)(2,1)} %fusion) | data formatting | bytes 16777216
  593.9 9.3 %copy.108 = bf16[16,128,16,128]{3,1,2,0:T(8,128)(2,1)} copy(bf16[16,128,16,128]{3,2,1,0:T(8,128)(2,1)} %bitcast.106) | data formatting | bytes 16777216 | tf_op jit(solution)/shard_map/reshape | solution.py:31
  603.2 12.0 %gather_fusion = bf16[256,128,128]{2,1,0:T(8,128)(2,1)} fusion(bf16[256,128,128]{2,1,0:T(8,128)(2,1)} %bitcast.105, s32[1024]{0:T(1024)S(1)} %pad_clamp_fusion), kind=kCustom, calls=%fused_computation.7 | custom fusion | bytes 16778240 | tf_op jit(solution)/shard_map/jit(_take)/gather | solution.py:59
  615.2 7.5 %multiply_bitcast_fusion = bf16[16,128,16,128]{3,1,2,0:T(8,128)(2,1)} fusion(bf16[16,16,128,128]{3,2,1,0:T(8,128)(2,1)} %bitcast.104, pred[16,16]{1,0:T(8,128)(4,1)S(1)} %compare_and_fusion, bf16[16,16]{1,0:T(8,128)(2,1)S(1)} %reshape.446), kind=kLoop, calls=%fused_computation.12 | loop fusion | flops 8388608 | bytes 16777984 | tf_op jit(solution)/shard_map/transpose | solution.py:40
  622.8 13.7 %copy.109 = bf16[16,128,16,128]{3,2,1,0:T(8,128)(2,1)} copy(bf16[16,128,16,128]{3,1,2,0:T(8,128)(2,1)} %multiply_bitcast_fusion) | data formatting | bytes 16777216 | tf_op jit(solution)/shard_map/transpose | solution.py:40
  636.4 11.1 %copy.136 = bf16[256,8,16,128]{3,1,2,0:T(8,128)(2,1)} copy(bf16[256,8,16,128]{3,2,1,0:T(8,128)(2,1)} %bitcast.107) | data formatting | bytes 16777216
  (139 shorter events, 25.6 us)
Async XLA Ops:
  7.2 202.4 %all-gather.21.cloned.1.call-start = ((), (), s32[]{:S(2)}) async-start(), calls=%async_computation.3 | async-start | bytes 10485760 | tf_op jit(solution)/shard_map/all_gather | solution.py:13
  34.3 303.1 %all-gather.17.cloned.1.call-start = ((), (), s32[]{:S(2)}) async-start(), calls=%async_computation.1 | async-start | bytes 10485760 | tf_op jit(solution)/shard_map/all_gather | solution.py:13
  45.4 3.6 copy-start.3
  47.2 380.1 %all-gather.19.cloned.1.call-start = ((), (), s32[]{:S(2)}) async-start(), calls=%async_computation.2 | async-start | bytes 18874368 | tf_op jit(solution)/shard_map/all_gather | solution.py:13
  62.6 456.1 %all-gather.15.cloned.1.call-start = ((), (), s32[]{:S(2)}) async-start(), calls=%async_computation | async-start | bytes 18874368 | tf_op jit(solution)/shard_map/all_gather | solution.py:13
  529.6 2.2 copy-start
  552.4 3.6 copy-start.2
  556.0 11.9 %copy-start.1 = (bf16[8,128,16,128]{3,2,1,0:T(8,128)(2,1)S(1)}, bf16[8,128,16,128]{3,2,1,0:T(8,128)(2,1)}, u32[]{:S(2)}) copy-start(bf16[8,128,16,128]{3,2,1,0:T(8,128)(2,1)} %copy.107) | copy-start | bytes 12582916
Sparse Core Ops, SparseCore 0:
  34.4 153.6 all-gather.20
  189.7 147.6 all-gather.16
  339.3 87.9 all-gather.18
  429.0 89.7 all-gather.14
